TPU v7x, 32 devices: a whole 2x2x4 slice. The times are simulated.
32 devices in a mesh: mkt: 4 (over z), draw: 4 (over y, core), nest: 2 (over x).
Axes of the slice: x: 2, y: 2, z: 4, core: 2. Of those that a mesh axis runs over, the one named last changes fastest.
Arguments:
- features: bfloat16 [32, 512, 128], P(None, 'mkt'), may hold values from -1.5 to 1.5
- taste_draws: bfloat16 [128, 32, 512], P('mkt', None, 'draw'), may hold values from -4 to 4
- taste_scale: float32 [32], replicated, may hold values from 0.2 to 1
- nest_param: float32 [16], P('nest'), may hold values from 0.3 to 0.95
- members: int32 [16, 48], P('nest'), may hold values from -1 to 511, as said below
- log_share: float32 [512, 128], P('mkt'), may hold values from -10 to -7
Outputs:
- mean_utility: float32 [128, 768], P('mkt', 'nest')
- model_share: float32 [128, 768], P('mkt', 'nest')
Inputs may be any that keep to these rules, and one draw needn't show every extreme that they name: `members`: every product id 0 to 511 stands in exactly one slot; in each nest's row the ids fill the first slots and -1 fills the rest; each nest holds at least 16 products, and some nest fills all 48 slots.
All inputs are finite; a program needn't handle non-finite values.
Results may differ from a plain program's by a relative error of at most 0.0013.
The roundings to bfloat16 on the way count: a program that leaves them out, or rounds other values in their place, can miss the bound.
Values may be sent and summed in bfloat16 or wider, within the bound.
A program may use at most 64 MiB of HBM per device.

v0:
```python
import jax
import jax.numpy as jnp
from jax import lax
from jax.sharding import PartitionSpec as P

ITERS = 3


def revise(value_slot, slot_share, target, nest_rate, occupied):
    safe_share = jnp.where(occupied[None, :], slot_share, 1.0)
    moved_value = value_slot + (1.0 - nest_rate)[None, :] * (target - jnp.log(safe_share))
    return jnp.where(occupied[None, :], moved_value, 0.0)


def shards(features, taste_draws, taste_scale, nest_param, members, log_share):
    market_x = lax.all_to_all(features, "mkt", split_axis=2, concat_axis=1, tiled=True)
    market_log = lax.all_to_all(log_share, "mkt", split_axis=1, concat_axis=0, tiled=True)
    market_list = market_log.shape[1]
    product_count = market_log.shape[0]
    nest_count = members.shape[0]
    slot_count = members.shape[1]
    columns = nest_count * slot_count
    draws_here = taste_draws.shape[2]
    total_draws = draws_here * lax.axis_size("draw")
    product_ids = members.reshape(columns)
    occupied = product_ids >= 0
    safe_ids = jnp.maximum(product_ids, 0)
    live_flag = occupied.astype(jnp.float32)
    product_range = jnp.arange(product_count, dtype=jnp.int32)
    onehot = ((safe_ids[None, :] == product_range[:, None]) & occupied[None, :]).astype(
        jnp.bfloat16
    )
    slot_features = jnp.einsum(
        "kjm,js->mks", market_x, onehot, preferred_element_type=jnp.float32
    ).astype(jnp.bfloat16)
    slot_log = jnp.transpose(jnp.take(market_log, safe_ids, axis=0), (1, 0))
    outside = 1.0 - jnp.sum(jnp.exp(market_log), axis=0)
    value_slot = jnp.where(occupied[None, :], slot_log - jnp.log(outside)[:, None], 0.0)
    taste_matrix = (taste_scale[None, :, None] * taste_draws.astype(jnp.float32)).astype(
        jnp.bfloat16
    )
    nest_rate = jnp.repeat(nest_param, slot_count)
    mean_utility_part = jnp.einsum(
        "dve,dvb->deb", slot_features, taste_matrix, preferred_element_type=jnp.float32
    )
    slot_share = jnp.zeros_like(value_slot)
    for iteration in range(ITERS):
        utility = live_flag[None, :, None] * jnp.exp(
            (value_slot[:, :, None] + mean_utility_part) / nest_rate[None, :, None]
        )
        grouped = utility.reshape(market_list, nest_count, slot_count, draws_here)
        inner_sum = jnp.sum(grouped, axis=2)
        inclusive_value = jnp.exp(nest_param[None, :, None] * jnp.log(inner_sum))
        totals = lax.psum(jnp.sum(inclusive_value, axis=1), "nest")
        nest_ratio = inclusive_value / (inner_sum * (1.0 + totals)[:, None, :])
        share_terms = jnp.sum(grouped * nest_ratio[:, :, None, :], axis=3).reshape(
            market_list, columns
        )
        slot_share = lax.psum(share_terms, "draw") / total_draws
        value_slot = revise(value_slot, slot_share, slot_log, nest_rate, occupied)
    return (value_slot, slot_share)


def solution(mesh):
    in_specs = (
        P(None, "mkt", None),
        P("mkt", None, "draw"),
        P(),
        P("nest"),
        P("nest", None),
        P("mkt", None),
    )
    out_specs = (P("mkt", "nest"), P("mkt", "nest"))
    return jax.shard_map(shards, mesh=mesh, in_specs=in_specs, out_specs=out_specs, check_vma=False)
```

profile of v0, /device:TPU:0, one launch (start us, length us, event | category | flops | bytes accessed | tf_op | source)
XLA Modules:
  0.0 170.6 jit_solution(5884183083681372627)
XLA Ops:
  0.7 1.6 copy.23
  2.2 6.3 %all-to-all-start = ((f32[128,4,32]{0,2,1:T(8,128)}), f32[128,4,32]{0,2,1:T(8,128)S(1)}, u32[]{:S(2)}, u32[]{:S(2)}) async-start(f32[128,4,32]{0,2,1:T(8,128)} %bitcast), calls=%async_computation | async-start | bytes 131072 | tf_op jit(solution)/shard_map/all_to_all | solution.py:17
  9.4 2.7 %copy.26 = bf16[32,128,128]{1,0,2:T(8,128)(2,1)} copy(bf16[32,128,128]{2,1,0:T(8,128)(2,1)} %param.6) | data formatting | bytes 2097152 | tf_op args[0]
  12.1 2.2 %all-to-all-done = f32[128,4,32]{0,2,1:T(8,128)S(1)} async-done(((f32[128,4,32]{0,2,1:T(8,128)}), f32[128,4,32]{0,2,1:T(8,128)S(1)}, u32[]{:S(2)}, u32[]{:S(2)}) %all-to-all-start) | async-done | bytes 65568 | tf_op jit(solution)/shard_map/all_to_all | solution.py:17
  14.3 3.5 %all-to-all-start.1 = ((bf16[32,128,128]{1,0,2:T(8,128)(2,1)}), bf16[32,128,128]{1,0,2:T(8,128)(2,1)S(1)}, u32[]{:S(2)}, u32[]{:S(2)}) async-start(bf16[32,128,128]{1,0,2:T(8,128)(2,1)} %copy.26), calls=%async_computation.1 | async-start | bytes 2097152 | tf_op jit(solution)/shard_map/all_to_all | solution.py:16
  21.1 21.3 %all-to-all-done.1 = bf16[32,128,128]{1,0,2:T(8,128)(2,1)S(1)} async-done(((bf16[32,128,128]{1,0,2:T(8,128)(2,1)}), bf16[32,128,128]{1,0,2:T(8,128)(2,1)S(1)}, u32[]{:S(2)}, u32[]{:S(2)}) %all-to-all-start.1) | async-done | bytes 1048608 | tf_op jit(solution)/shard_map/all_to_all | solution.py:16
  42.4 6.5 %exponential_multiply_fusion.2 = (f32[32,384,128]{2,1,0:T(8,128)}, f32[32,384,128]{2,1,0:T(8,128)}) fusion(f32[384]{0:T(512)S(1)} %reshape.109, f32[32,384]{1,0:T(8,128)S(1)} %copy.25, f32[384]{0:T(512)S(1)} %convert_element_type.20, bf16[32,32,128]{2,1,0:T(8,128)(2,1)S(1)} %copy-done.1, f32[32]{0:T(128)S(1)} %copy-done.2, ...), kind=kOutput, calls=%fused_computation.6 | convolution fusion | flops 509214720 | bytes 13947904 | tf_op jit(solution)/shard_map/dve,dvb->deb/dot_general | solution.py:43
  48.9 3.7 %reduce_sum.91 = f32[32,8,128]{2,1,0:T(8,128)S(1)} reduce(f32[32,8,48,128]{3,2,1,0:T(8,128)} %bitcast.62, f32[]{:T(128)} %constant.28.clone.1), dimensions={2}, to_apply=%region_1.2 | reduce | flops 1540096 | bytes 6422532 | tf_op jit(solution)/shard_map/reduce_sum | solution.py:52
  52.7 8.1 %psum.42 = f32[32,128]{1,0:T(8,128)S(1)} all-reduce(f32[32,128]{1,0:T(8,128)S(1)} %fusion.27), channel_id=1, replica_groups=mesh['mkt'=4,'draw'=4,'nest'=2] {'nest'}, use_global_device_ids=true, to_apply=%region_3.4 | all-reduce | flops 4096 | bytes 32768 | tf_op jit(solution)/shard_map/psum | solution.py:54
  61.0 6.2 %bitcast_multiply_fusion.2 = f32[32,384,128]{2,1,0:T(8,128)} fusion(f32[32,384,128]{2,1,0:T(8,128)} %get-tuple-element.10, f32[32,8,128]{2,1,0:T(8,128)S(1)} %multiply_divide_fusion.2), kind=kLoop, calls=%fused_computation.3 | loop fusion | flops 1572864 | bytes 12713984 | tf_op jit(solution)/shard_map/mul | solution.py:56
  67.2 4.5 %reduce_sum.93 = f32[32,384]{1,0:T(8,128)S(1)} reduce(f32[32,384,128]{2,1,0:T(8,128)} %bitcast_multiply_fusion.2, f32[]{:T(128)} %constant.28.clone.1), dimensions={2}, to_apply=%region_4.5 | reduce | flops 1560576 | bytes 6340612 | tf_op jit(solution)/shard_map/reduce_sum | solution.py:56
  71.8 12.0 %psum.43 = f32[32,384]{0,1:T(8,128)S(1)} all-reduce(f32[32,384]{0,1:T(8,128)S(1)} %copy.30), channel_id=1, replica_groups=mesh['mkt'=4,'draw'=4,'nest'=2] {'draw'}, use_global_device_ids=true, to_apply=%region_5.6 | all-reduce | flops 12288 | bytes 98304 | tf_op jit(solution)/shard_map/psum | solution.py:59
  84.1 6.8 %exponential_multiply_fusion.1 = f32[32,384,128]{2,1,0:T(8,128)} fusion(f32[32,384,128]{2,1,0:T(8,128)} %get-tuple-element.11, f32[32,384]{1,0:T(8,128)S(1)} %copy.31, f32[384]{0:T(512)S(1)} %reshape.109, f32[384]{0:T(512)S(1)} %convert_element_type.20), kind=kLoop, calls=%fused_computation.5 | loop fusion | flops 4718592 | bytes 12635136 | tf_op jit(solution)/shard_map/mul | solution.py:48
  90.9 3.7 %reduce_sum.94 = f32[32,8,128]{2,1,0:T(8,128)S(1)} reduce(f32[32,8,48,128]{3,2,1,0:T(8,128)} %bitcast.63, f32[]{:T(128)} %constant.28.clone.1), dimensions={2}, to_apply=%region_6.7 | reduce | flops 1540096 | bytes 6422532 | tf_op jit(solution)/shard_map/reduce_sum | solution.py:52
  94.7 7.2 %psum.44 = f32[32,128]{1,0:T(8,128)S(1)} all-reduce(f32[32,128]{1,0:T(8,128)S(1)} %fusion.26), channel_id=1, replica_groups=mesh['mkt'=4,'draw'=4,'nest'=2] {'nest'}, use_global_device_ids=true, to_apply=%region_8.9 | all-reduce | flops 4096 | bytes 32768 | tf_op jit(solution)/shard_map/psum | solution.py:54
  102.0 6.9 %bitcast_multiply_fusion.1 = f32[32,384,128]{2,1,0:T(8,128)} fusion(f32[32,8,128]{2,1,0:T(8,128)S(1)} %multiply_divide_fusion.1, f32[384]{0:T(512)S(1)} %reshape.109, f32[32,384,128]{2,1,0:T(8,128)} %get-tuple-element.11, f32[32,384]{1,0:T(8,128)S(1)} %copy.31, f32[384]{0:T(512)S(1)} %convert_element_type.20), kind=kLoop, calls=%fused_computation.2 | loop fusion | flops 6291456 | bytes 12766208 | tf_op jit(solution)/shard_map/mul | solution.py:56
  108.9 4.5 %reduce_sum.96 = f32[32,384]{1,0:T(8,128)S(1)} reduce(f32[32,384,128]{2,1,0:T(8,128)} %bitcast_multiply_fusion.1, f32[]{:T(128)} %constant.28.clone.1), dimensions={2}, to_apply=%region_9.10 | reduce | flops 1560576 | bytes 6340612 | tf_op jit(solution)/shard_map/reduce_sum | solution.py:56
  113.5 12.3 %psum.45 = f32[32,384]{0,1:T(8,128)S(1)} all-reduce(f32[32,384]{0,1:T(8,128)S(1)} %copy.32), channel_id=1, replica_groups=mesh['mkt'=4,'draw'=4,'nest'=2] {'draw'}, use_global_device_ids=true, to_apply=%region_10.11 | all-reduce | flops 12288 | bytes 98304 | tf_op jit(solution)/shard_map/psum | solution.py:59
  126.2 6.8 %exponential_multiply_fusion = f32[32,384,128]{2,1,0:T(8,128)} fusion(f32[32,384,128]{2,1,0:T(8,128)} %get-tuple-element.11, f32[32,384]{1,0:T(8,128)S(1)} %copy.33, f32[384]{0:T(512)S(1)} %reshape.109, f32[384]{0:T(512)S(1)} %convert_element_type.20), kind=kLoop, calls=%fused_computation.4 | loop fusion | flops 4718592 | bytes 12635136 | tf_op jit(solution)/shard_map/mul | solution.py:48
  133.0 3.7 %reduce_sum.97 = f32[32,8,128]{2,1,0:T(8,128)S(1)} reduce(f32[32,8,48,128]{3,2,1,0:T(8,128)} %bitcast.64, f32[]{:T(128)} %constant.28.clone.1), dimensions={2}, to_apply=%region_11.12 | reduce | flops 1540096 | bytes 6422532 | tf_op jit(solution)/shard_map/reduce_sum | solution.py:52
  136.7 8.1 %psum.46 = f32[32,128]{1,0:T(8,128)S(1)} all-reduce(f32[32,128]{1,0:T(8,128)S(1)} %fusion.25), channel_id=1, replica_groups=mesh['mkt'=4,'draw'=4,'nest'=2] {'nest'}, use_global_device_ids=true, to_apply=%region_13.14 | all-reduce | flops 4096 | bytes 32768 | tf_op jit(solution)/shard_map/psum | solution.py:54
  145.0 6.9 %bitcast_multiply_fusion = f32[32,384,128]{2,1,0:T(8,128)} fusion(f32[32,8,128]{2,1,0:T(8,128)S(1)} %multiply_divide_fusion, f32[384]{0:T(512)S(1)} %reshape.109, f32[32,384,128]{2,1,0:T(8,128)} %get-tuple-element.11, f32[32,384]{1,0:T(8,128)S(1)} %copy.33, f32[384]{0:T(512)S(1)} %convert_element_type.20), kind=kLoop, calls=%fused_computation.1 | loop fusion | flops 6291456 | bytes 12766208 | tf_op jit(solution)/shard_map/mul | solution.py:56
  151.9 4.5 %reduce_sum.99 = f32[32,384]{1,0:T(8,128)S(1)} reduce(f32[32,384,128]{2,1,0:T(8,128)} %bitcast_multiply_fusion, f32[]{:T(128)} %constant.28.clone.1), dimensions={2}, to_apply=%region_14.15 | reduce | flops 1560576 | bytes 6340612 | tf_op jit(solution)/shard_map/reduce_sum | solution.py:56
  156.5 12.4 %psum.47 = f32[32,384]{0,1:T(8,128)S(1)} all-reduce(f32[32,384]{0,1:T(8,128)S(1)} %copy.34), channel_id=1, replica_groups=mesh['mkt'=4,'draw'=4,'nest'=2] {'draw'}, use_global_device_ids=true, to_apply=%region_15.16 | all-reduce | flops 12288 | bytes 98304 | tf_op jit(solution)/shard_map/psum | solution.py:59
  (41 shorter events, 7.4 us)
Async XLA Ops:
  0.6 41.8 %copy-start.1 = (bf16[32,32,128]{2,1,0:T(8,128)(2,1)S(1)}, bf16[32,32,128]{2,1,0:T(8,128)(2,1)}, u32[]{:S(2)}) copy-start(bf16[32,32,128]{2,1,0:T(8,128)(2,1)} %param.7) | copy-start | bytes 786436
  0.6 41.8 %copy-start.2 = (f32[32]{0:T(128)S(1)}, f32[32]{0:T(128)}, u32[]{:S(2)}) copy-start(f32[32]{0:T(128)} %param.8) | copy-start | bytes 388
  2.2 12.1 %all-to-all-start = ((f32[128,4,32]{0,2,1:T(8,128)}), f32[128,4,32]{0,2,1:T(8,128)S(1)}, u32[]{:S(2)}, u32[]{:S(2)}) async-start(f32[128,4,32]{0,2,1:T(8,128)} %bitcast), calls=%async_computation | async-start | bytes 131072 | tf_op jit(solution)/shard_map/all_to_all | solution.py:17
  14.3 28.1 %all-to-all-start.1 = ((bf16[32,128,128]{1,0,2:T(8,128)(2,1)}), bf16[32,128,128]{1,0,2:T(8,128)(2,1)S(1)}, u32[]{:S(2)}, u32[]{:S(2)}) async-start(bf16[32,128,128]{1,0,2:T(8,128)(2,1)} %copy.26), calls=%async_computation.1 | async-start | bytes 2097152 | tf_op jit(solution)/shard_map/all_to_all | solution.py:16
  48.9 3.7 %copy-start = (f32[8]{0:T(128)S(1)}, f32[8]{0:T(128)}, u32[]{:S(2)}) copy-start(f32[8]{0:T(128)} %param.9) | copy-start | bytes 100
where the time goes:
time: 172 us; the launch traced here: 171 us
  other arithmetic  61.1 us (36%)
  blocking collectives  60.1 us (35%)
  waiting for transfers between devices  23.5 us (14%)
  starting transfers between devices  9.86 us (6%)
  local copies, waits for them, and re-layouts  8.63 us (5%)
  matrix products  6.49 us (4%)
    psum x3, blocking collectives, shards(): slot_share = lax.psum(share_terms, 'draw') / total_draws  36.7 us
    psum x3, blocking collectives, shards(): totals = lax.psum(jnp.sum(inclusive_value, axis=1), 'nest')  23.5 us
    all_to_all x1, waiting for transfers between devices, shards(): lax.all_to_all(features, 'mkt', split_axis=2, concat_axis=1, tiled=True)  21.3 us
    mul x3, other arithmetic, shards(): grouped * nest_ratio[:, :, None, :]  20.1 us
    mul x2, other arithmetic, shards(): live_flag[None, :, None]  13.6 us
    reduce_sum x3, other arithmetic, shards(): jnp.sum(grouped * nest_ratio[:, :, None, :], axis=3)  13.4 us
    reduce_sum x3, other arithmetic, shards(): inner_sum = jnp.sum(grouped, axis=2)  11 us
    dot_general x1, matrix products, shards(): jnp.einsum('dve,dvb->deb', slot_features, taste_matrix, preferred_element...  6.49 us
  transfers between devices with their start and end apart: 2, of which 2 were waited for; matrix products, arithmetic and copies ran while one was open for 4% of the time, Pallas kernels for 0%

commit v1 on v0

v1 whole, which is shorter than its diff:
```python
import functools
import math

import jax
import jax.numpy as jnp
from jax import lax
from jax.experimental import pallas as pl
from jax.experimental.pallas import tpu as pltpu
from jax.sharding import PartitionSpec as P

ITERS = 3
GROUP = 8
LANES = 128
LOG2E = math.log2(math.e)
EMPTY = -1e30
MESH = pl.DeviceIdType.MESH
F32 = jnp.float32
BF16 = jnp.bfloat16


def split3(x):
    hi = x.astype(BF16).astype(F32)
    rest = x - hi
    mid = rest.astype(BF16).astype(F32)
    return hi, mid, rest - mid


def kernel(
    n_nest, n_draw, total_draws,
    sx_ref, taste_ref, value0_ref, target_ref, rate_row_ref, live_row_ref, rate_col_ref, live_col_ref,
    value_ref, share_ref,
    mu_ref, u_ref, inner_ref, incl_ref, hi_ref, lo_ref, spread_ref, pick_ref, vcat_ref,
    tot_send, tot_recv, part_send, part_recv,
    tot_ssem, tot_rsem, part_ssem, part_rsem,
):
    markets, _, cols = sx_ref.shape
    draws = taste_ref.shape[2]
    nests = rate_col_ref.shape[0]
    slots = cols // nests
    chunks = markets // GROUP
    my_nest = lax.axis_index("nest")
    my_draw = lax.axis_index("draw")
    nest_peers = [lax.rem(my_nest + d, n_nest) for d in range(1, n_nest)]
    draw_peers = [lax.rem(my_draw + d, n_draw) for d in range(1, n_draw)]

    barrier = pltpu.get_barrier_semaphore()
    for peer in nest_peers:
        pl.semaphore_signal(barrier, inc=1, device_id={"nest": peer}, device_id_type=MESH)
    for peer in draw_peers:
        pl.semaphore_signal(barrier, inc=1, device_id={"draw": peer}, device_id_type=MESH)
    pl.semaphore_wait(barrier, n_nest + n_draw - 2)

    def tot_copy(it, ch, k):
        return pltpu.make_async_remote_copy(
            src_ref=tot_send.at[it, ch], dst_ref=tot_recv.at[it, ch, k],
            send_sem=tot_ssem.at[it, ch, k], recv_sem=tot_rsem.at[it, ch, k],
            device_id={"nest": nest_peers[k]}, device_id_type=MESH)

    def part_copy(it, ch, k):
        return pltpu.make_async_remote_copy(
            src_ref=part_send.at[it, ch], dst_ref=part_recv.at[it, ch, k],
            send_sem=part_ssem.at[it, ch, k], recv_sem=part_rsem.at[it, ch, k],
            device_id={"draw": draw_peers[k]}, device_id_type=MESH)

    row = lax.broadcasted_iota(jnp.int32, (LANES, draws), 0)
    lane = lax.broadcasted_iota(jnp.int32, (draws, LANES), 1)
    for i in range(GROUP):
        mine = (row == i) | (row == GROUP + i) | (row == 2 * GROUP + i)
        spread_ref[i] = jnp.where(mine, 1.0, 0.0).astype(BF16)
        pick_ref[i * draws:(i + 1) * draws, :] = jnp.where(lane == i, 1.0, 0.0).astype(BF16)

    rate_col = rate_col_ref[...]
    scale_col = LOG2E / rate_col
    rate_row = rate_row_ref[...]
    scale_row = LOG2E / rate_row
    live_row = live_row_ref[...]

    def mu_step(m, _):
        mu = lax.dot_general(sx_ref[m], taste_ref[m], (((0,), (0,)), ((), ())),
                             preferred_element_type=F32)
        mu = (mu.reshape(slots, nests, draws) * scale_col[None]).reshape(cols, draws)
        mu_ref[m] = jnp.where(live_col_ref[...] > 0.0, mu, EMPTY)
        return 0

    lax.fori_loop(0, markets, mu_step, 0)

    def utilities(it, ch, value):
        parts = split3(value * scale_row)
        stacked = jnp.concatenate(
            list(parts) + [jnp.zeros((LANES - 3 * GROUP, cols), F32)], axis=0)
        vcat_ref[...] = stacked.T.astype(BF16)

        def body(i, _):
            m = ch * GROUP + i
            shift = jnp.dot(vcat_ref[...], spread_ref[i], preferred_element_type=F32)
            u = jnp.exp2(mu_ref[m] + shift)
            u_ref[m] = u
            inner = jnp.sum(u.reshape(slots, nests, draws), axis=0)
            incl = jnp.exp(rate_col * jnp.log(inner))
            inner_ref[m] = inner
            incl_ref[m] = incl
            tot_send[it, ch, pl.ds(i, 1), :] = jnp.sum(incl, axis=0, keepdims=True)
            return 0

        lax.fori_loop(0, GROUP, body, 0)
        for k in range(n_nest - 1):
            tot_copy(it, ch, k).start()

    def shares(it, ch):
        for k in range(n_nest - 1):
            tot_copy(it, ch, k).wait_recv()

        def body(i, _):
            m = ch * GROUP + i
            total = 1.0 + tot_send[it, ch, pl.ds(i, 1), :]
            for k in range(n_nest - 1):
                total = total + tot_recv[it, ch, k, pl.ds(i, 1), :]
            ratio = incl_ref[m] / (inner_ref[m] * total)
            p = (u_ref[m].reshape(slots, nests, draws) * ratio[None]).reshape(cols, draws)
            hi = p.astype(BF16)
            at = pl.ds(pl.multiple_of(i * draws, draws), draws)
            hi_ref[:, at] = hi
            lo_ref[:, at] = (p - hi.astype(F32)).astype(BF16)
            return 0

        lax.fori_loop(0, GROUP, body, 0)
        out = jnp.dot(hi_ref[...], pick_ref[...], preferred_element_type=F32)
        out = out + jnp.dot(lo_ref[...], pick_ref[...], preferred_element_type=F32)
        part_send[it, ch] = out.T[:GROUP]
        for k in range(n_draw - 1):
            part_copy(it, ch, k).start()

    def update(it, ch):
        for k in range(n_draw - 1):
            part_copy(it, ch, k).wait_recv()
        share = part_send[it, ch]
        for k in range(n_draw - 1):
            share = share + part_recv[it, ch, k]
        share = share * (1.0 / total_draws)
        rows = pl.ds(pl.multiple_of(ch * GROUP, GROUP), GROUP)
        value = value_ref[rows, :]
        moved = value + (1.0 - rate_row) * (
            target_ref[rows, :] - jnp.log(jnp.where(live_row > 0.0, share, 1.0)))
        value = jnp.where(live_row > 0.0, moved, 0.0)
        value_ref[rows, :] = value
        if it == ITERS - 1:
            share_ref[rows, :] = share
        else:
            utilities(it + 1, ch, value)

    value_ref[...] = value0_ref[...]

    def each(fn):
        def step(ch, _):
            fn(ch)
            return 0
        lax.fori_loop(0, chunks, step, 0)

    each(lambda ch: utilities(0, ch, value_ref[pl.ds(pl.multiple_of(ch * GROUP, GROUP), GROUP), :]))
    for it in range(ITERS):
        each(functools.partial(shares, it))
        each(functools.partial(update, it))

    def drain(ch):
        for it in range(ITERS):
            for k in range(n_nest - 1):
                tot_copy(it, ch, k).wait_send()
            for k in range(n_draw - 1):
                part_copy(it, ch, k).wait_send()

    each(drain)


def iterate(sx, taste, value0, target, rate_row, live_row, rate_col, live_col, total_draws):
    markets, _, cols = sx.shape
    draws = taste.shape[2]
    nests = rate_col.shape[0]
    chunks = markets // GROUP
    n_nest = lax.axis_size("nest")
    n_draw = lax.axis_size("draw")
    vm = pl.BlockSpec(memory_space=pltpu.VMEM)
    return pl.pallas_call(
        functools.partial(kernel, n_nest, n_draw, total_draws),
        out_shape=[jax.ShapeDtypeStruct((markets, cols), F32)] * 2,
        in_specs=[vm] * 8,
        out_specs=[vm] * 2,
        scratch_shapes=[
            pltpu.VMEM((markets, cols, draws), F32),
            pltpu.VMEM((markets, cols, draws), F32),
            pltpu.VMEM((markets, nests, draws), F32),
            pltpu.VMEM((markets, nests, draws), F32),
            pltpu.VMEM((cols, GROUP * draws), BF16),
            pltpu.VMEM((cols, GROUP * draws), BF16),
            pltpu.VMEM((GROUP, LANES, draws), BF16),
            pltpu.VMEM((GROUP * draws, LANES), BF16),
            pltpu.VMEM((cols, LANES), BF16),
            pltpu.VMEM((ITERS, chunks, GROUP, draws), F32),
            pltpu.VMEM((ITERS, chunks, n_nest - 1, GROUP, draws), F32),
            pltpu.VMEM((ITERS, chunks, GROUP, cols), F32),
            pltpu.VMEM((ITERS, chunks, n_draw - 1, GROUP, cols), F32),
            pltpu.SemaphoreType.DMA((ITERS, chunks, n_nest - 1)),
            pltpu.SemaphoreType.DMA((ITERS, chunks, n_nest - 1)),
            pltpu.SemaphoreType.DMA((ITERS, chunks, n_draw - 1)),
            pltpu.SemaphoreType.DMA((ITERS, chunks, n_draw - 1)),
        ],
        compiler_params=pltpu.CompilerParams(
            collective_id=0, has_side_effects=True, vmem_limit_bytes=50 * 1024 * 1024),
        name="iterate",
    )(sx, taste, value0, target, rate_row, live_row, rate_col, live_col)


def shards(features, taste_draws, taste_scale, nest_param, members, log_share):
    market_x = lax.all_to_all(features, "mkt", split_axis=2, concat_axis=1, tiled=True)
    market_log = lax.all_to_all(log_share, "mkt", split_axis=1, concat_axis=0, tiled=True)
    markets = market_log.shape[1]
    products = market_log.shape[0]
    nests, slots = members.shape
    columns = nests * slots
    draws = taste_draws.shape[2]
    total_draws = draws * lax.axis_size("draw")
    ids = members.T.reshape(columns)
    occupied = ids >= 0
    safe_ids = jnp.maximum(ids, 0)
    onehot = (ids[None, :] == jnp.arange(products, dtype=jnp.int32)[:, None]).astype(BF16)
    sx = jnp.einsum("kjm,js->mks", market_x, onehot, preferred_element_type=F32).astype(BF16)
    target = jnp.transpose(jnp.take(market_log, safe_ids, axis=0), (1, 0))
    outside = 1.0 - jnp.sum(jnp.exp(market_log), axis=0)
    value0 = jnp.where(occupied[None, :], target - jnp.log(outside)[:, None], 0.0)
    taste = (taste_scale[None, :, None] * taste_draws.astype(F32)).astype(BF16)
    rate_row = jnp.tile(nest_param, slots)[None, :]
    live_row = occupied.astype(F32)[None, :]
    rate_col = jnp.broadcast_to(nest_param[:, None], (nests, draws))
    live_col = jnp.broadcast_to(occupied.astype(F32)[:, None], (columns, draws))
    value, share = iterate(sx, taste, value0, target, rate_row, live_row, rate_col, live_col, total_draws)

    def order(x):
        return x.reshape(markets, slots, nests).transpose(0, 2, 1).reshape(markets, columns)

    return order(value), order(share)


def solution(mesh):
    in_specs = (
        P(None, "mkt", None),
        P("mkt", None, "draw"),
        P(),
        P("nest"),
        P("nest", None),
        P("mkt", None),
    )
    out_specs = (P("mkt", "nest"), P("mkt", "nest"))
    return jax.shard_map(shards, mesh=mesh, in_specs=in_specs, out_specs=out_specs, check_vma=False)
```

time: 172 us -> 97.2 us (0.57)
  other arithmetic: 61.1 us -> 0.36 us
  blocking collectives: 60.1 us -> 0 us
  Pallas kernels: 0 us -> 49.4 us
  matrix products: 6.49 us -> 0.74 us
  local copies, waits for them, and re-layouts: 8.63 us -> 10.5 us
    psum x6 -> x0, blocking collectives: 60.1 us -> none  [the longest x3 36.7 us: shards(): slot_share = lax.psum(share_terms, 'draw') / total_draws]
    pallas_call x0 -> x1, Pallas kernels: none -> 49.4 us  [iterate(): pl.pallas_call(functools.partial(kernel, n_nest, n_draw, total_draws), ou...]
    mul x5 -> x0, other arithmetic: 33.7 us -> none  [the longest x3 20.1 us: shards(): grouped * nest_ratio[:, :, None, :]]
    reduce_sum x9 -> x0, other arithmetic: 24.8 us -> none  [the longest x3 13.4 us: shards(): jnp.sum(grouped * nest_ratio[:, :, None, :], axis=3)]
    dot_general x1 -> x0, matrix products: 6.49 us -> none  [shards(): jnp.einsum('dve,dvb->deb', slot_features, taste_matrix, preferred_element...]
  transfers between devices with their start and end apart: 2 -> 2, of which waited for: 2 -> 2; matrix products, arithmetic and copies ran while one was open for 4% -> 5% of each run, Pallas kernels for 0% -> 0%
where the time goes in v1:
time: 97.2 us; the launch traced here: 96.8 us
  Pallas kernels  49.4 us (51%)
  waiting for transfers between devices  25.2 us (26%)
  local copies, waits for them, and re-layouts  10.5 us (11%)
  starting transfers between devices  9.86 us (10%)
    pallas_call x1, Pallas kernels, iterate(): pl.pallas_call(functools.partial(kernel, n_nest, n_draw, total_draws), ou...  49.4 us
    all_to_all x1, waiting for transfers between devices, shards(): lax.all_to_all(features, 'mkt', split_axis=2, concat_axis=1, tiled=True)  22.3 us
    all_to_all x1, starting transfers between devices, shards(): lax.all_to_all(log_share, 'mkt', split_axis=1, concat_axis=0, tiled=True)  6.35 us
    unnamed x10, local copies, waits for them, and re-layouts  4.25 us
    all_to_all x1, starting transfers between devices, shards(): lax.all_to_all(features, 'mkt', split_axis=2, concat_axis=1, tiled=True)  3.52 us
    all_to_all x1, waiting for transfers between devices, shards(): lax.all_to_all(log_share, 'mkt', split_axis=1, concat_axis=0, tiled=True)  2.89 us
  transfers between devices with their start and end apart: 2, of which 2 were waited for; matrix products, arithmetic and copies ran while one was open for 5% of the time, Pallas kernels for 0%

profile of v1, /device:TPU:0, one launch (start us, length us, event | category | flops | bytes accessed | tf_op | source)
XLA Modules:
  0.0 96.8 jit_solution(18197135191838699790)
XLA Ops:
  0.6 1.6 %copy.44 = f32[128,128]{0,1:T(8,128)} copy(f32[128,128]{1,0:T(8,128)} %param.11) | data formatting | bytes 131072 | tf_op args[5]
  2.2 6.3 %all-to-all-start.1 = ((f32[128,4,32]{0,2,1:T(8,128)}), f32[128,4,32]{0,2,1:T(8,128)S(1)}, u32[]{:S(2)}, u32[]{:S(2)}) async-start(f32[128,4,32]{0,2,1:T(8,128)} %bitcast.8), calls=%async_computation.1 | async-start | bytes 131072 | tf_op jit(solution)/shard_map/all_to_all | solution.py:214
  8.6 2.7 %copy.40 = bf16[32,128,128]{1,0,2:T(8,128)(2,1)} copy(bf16[32,128,128]{2,1,0:T(8,128)(2,1)} %param.6) | data formatting | bytes 2097152 | tf_op args[0]
  11.4 2.9 %all-to-all-done.1 = f32[128,4,32]{0,2,1:T(8,128)S(1)} async-done(((f32[128,4,32]{0,2,1:T(8,128)}), f32[128,4,32]{0,2,1:T(8,128)S(1)}, u32[]{:S(2)}, u32[]{:S(2)}) %all-to-all-start.1) | async-done | bytes 65568 | tf_op jit(solution)/shard_map/all_to_all | solution.py:214
  14.3 3.5 %all-to-all-start = ((bf16[32,128,128]{1,0,2:T(8,128)(2,1)}), bf16[32,128,128]{1,0,2:T(8,128)(2,1)S(1)}, u32[]{:S(2)}, u32[]{:S(2)}) async-start(bf16[32,128,128]{1,0,2:T(8,128)(2,1)} %copy.40), calls=%async_computation | async-start | bytes 2097152 | tf_op jit(solution)/shard_map/all_to_all | solution.py:213
  18.2 0.1 reshape.76.live_row_ref
  18.3 0.1 multiply_convert_fusion.taste_ref
  18.5 0.1 copy.45
  18.6 1.1 %gather_fusion = f32[384,32]{1,0:T(8,128)S(1)} fusion(f32[512,32]{1,0:T(8,128)S(1)} %bitcast.30, s32[1024]{0:T(1024)S(1)} %pad_clamp_fusion), kind=kCustom, calls=%fused_computation | custom fusion | bytes 99840 | tf_op jit(solution)/shard_map/jit(_take)/gather | solution.py:226
  19.7 0.1 copy.47
  19.8 0.1 exponential_reduce_fusion
  20.1 22.3 %all-to-all-done = bf16[32,128,128]{1,0,2:T(8,128)(2,1)S(1)} async-done(((bf16[32,128,128]{1,0,2:T(8,128)(2,1)}), bf16[32,128,128]{1,0,2:T(8,128)(2,1)S(1)}, u32[]{:S(2)}, u32[]{:S(2)}) %all-to-all-start) | async-done | bytes 1048608 | tf_op jit(solution)/shard_map/all_to_all | solution.py:213
  42.4 0.8 copy.42
  43.2 0.4 all_to_all.30
  43.6 0.7 fusion.1
  44.4 0.9 copy.57
  45.3 0.1 broadcast_in_dim.44.live_col_ref
  45.4 49.4 %iterate.1 = (f32[32,384]{1,0:T(8,128)S(1)}, f32[32,384]{1,0:T(8,128)S(1)}) custom-call(bf16[32,32,384]{2,1,0:T(8,128)(2,1)S(1)} %bitcast.29, bf16[32,32,128]{2,1,0:T(8,128)(2,1)S(1)} %multiply_convert_fusion.taste_ref, f32[32,384]{1,0:T(8,128)S(1)} %get-tuple-element.8.value0_ref, f32[32,384]{1,0:T(8,128)S(1)} %get-tuple-element.9.target_ref, ...), custom_call_target="tpu_custom_call" | custom-call | tf_op jit(solution)/shard_map/iterate/pallas_call | solution.py:182
  94.8 0.1 copy.49
  94.9 0.1 copy.50
  95.1 0.7 reshape.73
  95.8 0.1 copy.51
  95.9 0.1 copy.52
  96.1 0.7 reshape.75
  (22 shorter events, 0.7 us)
Async XLA Ops:
  0.6 10.6 %copy-start.1 = (s32[8,48]{1,0:T(8,128)S(1)}, s32[8,48]{1,0:T(8,128)}, u32[]{:S(2)}) copy-start(s32[8,48]{1,0:T(8,128)} %param.10) | copy-start | bytes 4612
  2.2 12.1 %all-to-all-start.1 = ((f32[128,4,32]{0,2,1:T(8,128)}), f32[128,4,32]{0,2,1:T(8,128)S(1)}, u32[]{:S(2)}, u32[]{:S(2)}) async-start(f32[128,4,32]{0,2,1:T(8,128)} %bitcast.8), calls=%async_computation.1 | async-start | bytes 131072 | tf_op jit(solution)/shard_map/all_to_all | solution.py:214
  11.2 6.8 %copy-start.2 = (f32[8]{0:T(128)S(1)}, f32[8]{0:T(128)}, u32[]{:S(2)}) copy-start(f32[8]{0:T(128)} %param.9) | copy-start | bytes 100
  11.2 7.1 %copy-start = (bf16[32,32,128]{2,1,0:T(8,128)(2,1)S(1)}, bf16[32,32,128]{2,1,0:T(8,128)(2,1)}, u32[]{:S(2)}) copy-start(bf16[32,32,128]{2,1,0:T(8,128)(2,1)} %param.7) | copy-start | bytes 786436
  11.2 7.1 %copy-start.3 = (f32[32]{0:T(128)S(1)}, f32[32]{0:T(128)}, u32[]{:S(2)}) copy-start(f32[32]{0:T(128)} %param.8) | copy-start | bytes 388
  14.3 28.1 %all-to-all-start = ((bf16[32,128,128]{1,0,2:T(8,128)(2,1)}), bf16[32,128,128]{1,0,2:T(8,128)(2,1)S(1)}, u32[]{:S(2)}, u32[]{:S(2)}) async-start(bf16[32,128,128]{1,0,2:T(8,128)(2,1)} %copy.40), calls=%async_computation | async-start | bytes 2097152 | tf_op jit(solution)/shard_map/all_to_all | solution.py:213

commit v2 on v1

--- a/solution.py
+++ b/solution.py
@@ -26,29 +26,83 @@
 
 
 def kernel(
-    n_nest, n_draw, total_draws,
-    sx_ref, taste_ref, value0_ref, target_ref, rate_row_ref, live_row_ref, rate_col_ref, live_col_ref,
+    n_mkt, n_nest, n_draw, total_draws,
+    feat_ref, log_ref, taste_ref, scale_ref, ids_ref, param_ref,
     value_ref, share_ref,
+    x_ref, logm_ref, onehot_ref, s_ref, target_ref, live_col_ref,
     mu_ref, u_ref, inner_ref, incl_ref, hi_ref, lo_ref, spread_ref, pick_ref, vcat_ref,
     tot_send, tot_recv, part_send, part_recv,
+    own_sem, z_ssem, z_rsem, log_ssem, log_rsem, x_ssem, x_rsem, c_ssem, c_rsem,
     tot_ssem, tot_rsem, part_ssem, part_rsem,
 ):
-    markets, _, cols = sx_ref.shape
-    draws = taste_ref.shape[2]
-    nests = rate_col_ref.shape[0]
+    markets, depth, draws = taste_ref.shape
+    cols = ids_ref.shape[1]
+    nests = param_ref.shape[0]
+    products = feat_ref.shape[3]
     slots = cols // nests
     chunks = markets // GROUP
+    block = feat_ref.shape[1]
+    my_mkt = lax.axis_index("mkt")
     my_nest = lax.axis_index("nest")
     my_draw = lax.axis_index("draw")
+    mkt_peers = [lax.rem(my_mkt + d, n_mkt) for d in range(1, n_mkt)]
     nest_peers = [lax.rem(my_nest + d, n_nest) for d in range(1, n_nest)]
     draw_peers = [lax.rem(my_draw + d, n_draw) for d in range(1, n_draw)]
+    half = lax.rem(my_draw, 2)
+    partner = my_draw + 1 - 2 * half
 
     barrier = pltpu.get_barrier_semaphore()
-    for peer in nest_peers:
-        pl.semaphore_signal(barrier, inc=1, device_id={"nest": peer}, device_id_type=MESH)
-    for peer in draw_peers:
-        pl.semaphore_signal(barrier, inc=1, device_id={"draw": peer}, device_id_type=MESH)
-    pl.semaphore_wait(barrier, n_nest + n_draw - 2)
+    for axis, peers in (("mkt", mkt_peers), ("nest", nest_peers), ("draw", draw_peers)):
+        for peer in peers:
+            pl.semaphore_signal(barrier, inc=1, device_id={axis: peer}, device_id_type=MESH)
+
+    def here(source, nest):
+        return x_ref.at[source, pl.ds((2 * nest + half) * block, block)]
+
+    def z_copy(d):
+        return pltpu.make_async_remote_copy(
+            src_ref=feat_ref.at[mkt_peers[d - 1]], dst_ref=here(my_mkt, my_nest),
+            send_sem=z_ssem.at[d], recv_sem=z_rsem.at[d],
+            device_id={"mkt": mkt_peers[d - 1]}, device_id_type=MESH)
+
+    def log_copy(d):
+        return pltpu.make_async_remote_copy(
+            src_ref=log_ref.at[mkt_peers[d - 1]], dst_ref=logm_ref.at[my_mkt],
+            send_sem=log_ssem.at[d], recv_sem=log_rsem.at[d],
+            device_id={"mkt": mkt_peers[d - 1]}, device_id_type=MESH)
+
+    def origin(d):
+        return lax.rem(my_mkt + n_mkt - d, n_mkt)
+
+    def own_block(d):
+        return feat_ref.at[my_mkt] if d == 0 else here(origin(d), my_nest)
+
+    def x_copy(d, k):
+        return pltpu.make_async_remote_copy(
+            src_ref=own_block(d), dst_ref=here(origin(d), my_nest),
+            send_sem=x_ssem.at[d, k], recv_sem=x_rsem.at[d, k],
+            device_id={"nest": nest_peers[k]}, device_id_type=MESH)
+
+    def c_copy(d, k):
+        nest = my_nest if k == 0 else lax.rem(my_nest + n_nest - k, n_nest)
+        src = own_block(d) if k == 0 else here(origin(d), nest)
+        return pltpu.make_async_remote_copy(
+            src_ref=src, dst_ref=here(origin(d), nest),
+            send_sem=c_ssem.at[d, k], recv_sem=c_rsem.at[d, k],
+            device_id={"draw": partner}, device_id_type=MESH)
+
+    own_x = pltpu.make_async_copy(feat_ref.at[my_mkt], here(my_mkt, my_nest), own_sem.at[0])
+    own_log = pltpu.make_async_copy(log_ref.at[my_mkt], logm_ref.at[my_mkt], own_sem.at[1])
+    own_x.start()
+    own_log.start()
+    pl.semaphore_wait(barrier, n_mkt + n_nest + n_draw - 3)
+    for d in range(1, n_mkt):
+        z_copy(d).start()
+    for k in range(n_nest - 1):
+        x_copy(0, k).start()
+    c_copy(0, 0).start()
+    for d in range(1, n_mkt):
+        log_copy(d).start()
 
     def tot_copy(it, ch, k):
         return pltpu.make_async_remote_copy(
@@ -69,20 +123,64 @@
         spread_ref[i] = jnp.where(mine, 1.0, 0.0).astype(BF16)
         pick_ref[i * draws:(i + 1) * draws, :] = jnp.where(lane == i, 1.0, 0.0).astype(BF16)
 
-    rate_col = rate_col_ref[...]
+    ids = ids_ref[...]
+    live_row = jnp.where(ids >= 0, 1.0, 0.0)
+    live_col_ref[...] = jnp.broadcast_to(live_row, (draws, cols)).T
+    rate_col = jnp.broadcast_to(param_ref[...], (nests, draws))
     scale_col = LOG2E / rate_col
-    rate_row = rate_row_ref[...]
+    rate_row = jnp.broadcast_to(rate_col[None], (slots, nests, draws)).reshape(cols, draws).T[:1]
     scale_row = LOG2E / rate_row
-    live_row = live_row_ref[...]
+    product = lax.broadcasted_iota(jnp.int32, (products, cols), 0)
+    for z in range(n_mkt):
+        onehot_ref[z] = jnp.where(ids - z * products == product, 1.0, 0.0).astype(BF16)
+
+    for d in range(n_mkt):
+        if d == 0:
+            own_x.wait()
+        else:
+            z_copy(d).wait_recv()
+            for k in range(n_nest - 1):
+                x_copy(d, k).start()
+            c_copy(d, 0).start()
+        for k in range(n_nest - 1):
+            x_copy(d, k).wait_recv()
+            c_copy(d, k + 1).start()
+    for d in range(n_mkt):
+        for k in range(n_nest):
+            c_copy(d, k).wait_recv()
+        source = origin(d)
+        part = jnp.dot(x_ref[source].reshape(depth * markets, products), onehot_ref[source],
+                       preferred_element_type=F32)
+        for w in range(cols // LANES):
+            piece = part[:, w * LANES:(w + 1) * LANES]
+            if d == 0:
+                s_ref[w] = piece
+            else:
+                s_ref[w] += piece
 
     def mu_step(m, _):
-        mu = lax.dot_general(sx_ref[m], taste_ref[m], (((0,), (0,)), ((), ())),
-                             preferred_element_type=F32)
+        rows = pl.ds(m, depth, stride=markets)
+        sx = jnp.concatenate([s_ref.at[w][rows, :] for w in range(cols // LANES)], axis=1).astype(BF16)
+        taste = (scale_ref[...] * taste_ref[m].astype(F32)).astype(BF16)
+        mu = lax.dot_general(sx, taste, (((0,), (0,)), ((), ())), preferred_element_type=F32)
         mu = (mu.reshape(slots, nests, draws) * scale_col[None]).reshape(cols, draws)
         mu_ref[m] = jnp.where(live_col_ref[...] > 0.0, mu, EMPTY)
         return 0
 
     lax.fori_loop(0, markets, mu_step, 0)
+
+    own_log.wait()
+    for d in range(1, n_mkt):
+        log_copy(d).wait_recv()
+    target = jnp.zeros((markets, cols), F32)
+    inside = jnp.zeros((markets, 1), F32)
+    for z in range(n_mkt):
+        logs = logm_ref[z]
+        inside = inside + jnp.sum(jnp.exp(logs), axis=1, keepdims=True)
+        for term in split3(logs):
+            target = target + jnp.dot(term.astype(BF16), onehot_ref[z], preferred_element_type=F32)
+    target_ref[...] = target
+    value_ref[...] = jnp.where(live_row > 0.0, target - jnp.log(1.0 - inside), 0.0)
 
     def utilities(it, ch, value):
         parts = split3(value * scale_row)
@@ -148,8 +246,6 @@
         else:
             utilities(it + 1, ch, value)
 
-    value_ref[...] = value0_ref[...]
-
     def each(fn):
         def step(ch, _):
             fn(ch)
@@ -169,22 +265,39 @@
                 part_copy(it, ch, k).wait_send()
 
     each(drain)
-
-
-def iterate(sx, taste, value0, target, rate_row, live_row, rate_col, live_col, total_draws):
-    markets, _, cols = sx.shape
-    draws = taste.shape[2]
-    nests = rate_col.shape[0]
-    chunks = markets // GROUP
+    for d in range(n_mkt):
+        if d > 0:
+            z_copy(d).wait_send()
+            log_copy(d).wait_send()
+        for k in range(n_nest - 1):
+            x_copy(d, k).wait_send()
+        for k in range(n_nest):
+            c_copy(d, k).wait_send()
+
+
+def iterate(feat, logs, taste, scale, ids, param, total_draws):
+    n_mkt = lax.axis_size("mkt")
     n_nest = lax.axis_size("nest")
     n_draw = lax.axis_size("draw")
+    markets, depth, draws = taste.shape
+    cols = ids.shape[1]
+    nests = param.shape[0]
+    products = feat.shape[3]
+    chunks = markets // GROUP
     vm = pl.BlockSpec(memory_space=pltpu.VMEM)
+    dma = pltpu.SemaphoreType.DMA
     return pl.pallas_call(
-        functools.partial(kernel, n_nest, n_draw, total_draws),
+        functools.partial(kernel, n_mkt, n_nest, n_draw, total_draws),
         out_shape=[jax.ShapeDtypeStruct((markets, cols), F32)] * 2,
-        in_specs=[vm] * 8,
+        in_specs=[vm] * 6,
         out_specs=[vm] * 2,
         scratch_shapes=[
+            pltpu.VMEM((n_mkt, depth, markets, products), BF16),
+            pltpu.VMEM((n_mkt, markets, products), F32),
+            pltpu.VMEM((n_mkt, products, cols), BF16),
+            pltpu.VMEM((cols // LANES, depth * markets, LANES), F32),
+            pltpu.VMEM((markets, cols), F32),
+            pltpu.VMEM((cols, draws), F32),
             pltpu.VMEM((markets, cols, draws), F32),
             pltpu.VMEM((markets, cols, draws), F32),
             pltpu.VMEM((markets, nests, draws), F32),
@@ -198,40 +311,35 @@
             pltpu.VMEM((ITERS, chunks, n_nest - 1, GROUP, draws), F32),
             pltpu.VMEM((ITERS, chunks, GROUP, cols), F32),
             pltpu.VMEM((ITERS, chunks, n_draw - 1, GROUP, cols), F32),
-            pltpu.SemaphoreType.DMA((ITERS, chunks, n_nest - 1)),
-            pltpu.SemaphoreType.DMA((ITERS, chunks, n_nest - 1)),
-            pltpu.SemaphoreType.DMA((ITERS, chunks, n_draw - 1)),
-            pltpu.SemaphoreType.DMA((ITERS, chunks, n_draw - 1)),
+            dma((2,)),
+            dma((n_mkt,)), dma((n_mkt,)), dma((n_mkt,)), dma((n_mkt,)),
+            dma((n_mkt, n_nest - 1)), dma((n_mkt, n_nest - 1)),
+            dma((n_mkt, n_nest)), dma((n_mkt, n_nest)),
+            dma((ITERS, chunks, n_nest - 1)), dma((ITERS, chunks, n_nest - 1)),
+            dma((ITERS, chunks, n_draw - 1)), dma((ITERS, chunks, n_draw - 1)),
         ],
         compiler_params=pltpu.CompilerParams(
             collective_id=0, has_side_effects=True, vmem_limit_bytes=50 * 1024 * 1024),
         name="iterate",
-    )(sx, taste, value0, target, rate_row, live_row, rate_col, live_col)
+    )(feat, logs, taste, scale, ids, param)
 
 
 def shards(features, taste_draws, taste_scale, nest_param, members, log_share):
-    market_x = lax.all_to_all(features, "mkt", split_axis=2, concat_axis=1, tiled=True)
-    market_log = lax.all_to_all(log_share, "mkt", split_axis=1, concat_axis=0, tiled=True)
-    markets = market_log.shape[1]
-    products = market_log.shape[0]
+    n_mkt = lax.axis_size("mkt")
+    depth, products, all_markets = features.shape
+    markets = all_markets // n_mkt
     nests, slots = members.shape
     columns = nests * slots
     draws = taste_draws.shape[2]
     total_draws = draws * lax.axis_size("draw")
-    ids = members.T.reshape(columns)
-    occupied = ids >= 0
-    safe_ids = jnp.maximum(ids, 0)
-    onehot = (ids[None, :] == jnp.arange(products, dtype=jnp.int32)[:, None]).astype(BF16)
-    sx = jnp.einsum("kjm,js->mks", market_x, onehot, preferred_element_type=F32).astype(BF16)
-    target = jnp.transpose(jnp.take(market_log, safe_ids, axis=0), (1, 0))
-    outside = 1.0 - jnp.sum(jnp.exp(market_log), axis=0)
-    value0 = jnp.where(occupied[None, :], target - jnp.log(outside)[:, None], 0.0)
-    taste = (taste_scale[None, :, None] * taste_draws.astype(F32)).astype(BF16)
-    rate_row = jnp.tile(nest_param, slots)[None, :]
-    live_row = occupied.astype(F32)[None, :]
-    rate_col = jnp.broadcast_to(nest_param[:, None], (nests, draws))
-    live_col = jnp.broadcast_to(occupied.astype(F32)[:, None], (columns, draws))
-    value, share = iterate(sx, taste, value0, target, rate_row, live_row, rate_col, live_col, total_draws)
+    block = depth // (2 * lax.axis_size("nest"))
+    at = (2 * lax.axis_index("nest") + lax.rem(lax.axis_index("draw"), 2)) * block
+    feat = lax.dynamic_slice_in_dim(features, at, block, axis=0)
+    feat = feat.reshape(block, products, n_mkt, markets).transpose(2, 0, 3, 1)
+    logs = log_share.reshape(products, n_mkt, markets).transpose(1, 2, 0)
+    scale = jnp.broadcast_to(taste_scale[:, None], (depth, draws))
+    ids = members.T.reshape(1, columns)
+    value, share = iterate(feat, logs, taste_draws, scale, ids, nest_param[:, None], total_draws)
 
     def order(x):
         return x.reshape(markets, slots, nests).transpose(0, 2, 1).reshape(markets, columns)

time: 97.2 us -> 78 us (0.80)
  waiting for transfers between devices: 25.2 us -> 0 us
  Pallas kernels: 49.4 us -> 70.6 us
  starting transfers between devices: 9.86 us -> 0 us
  local copies, waits for them, and re-layouts: 10.5 us -> 6.42 us
    all_to_all x2 -> x0, waiting for transfers between devices: 25.2 us -> none  [the longest x1 22.3 us: shards(): lax.all_to_all(features, 'mkt', split_axis=2, concat_axis=1, tiled=True)]
    pallas_call x1, Pallas kernels: 49.4 us -> 70.6 us  [iterate(): pl.pallas_call(functools.partial(kernel, n_mkt, n_nest, n_draw, total_dra...]
    all_to_all x2 -> x0, starting transfers between devices: 9.86 us -> none  [the longest x1 6.35 us: shards(): lax.all_to_all(log_share, 'mkt', split_axis=1, concat_axis=0, tiled=True)]
    all_to_all x3 -> x0, local copies, waits for them, and re-layouts: 1.38 us -> none  [the longest x2 1.25 us: shards(): lax.all_to_all(features, 'mkt', split_axis=2, concat_axis=1, tiled=True)]
    gather x2 -> x0, local copies, waits for them, and re-layouts: 1.22 us -> none  [shards(): target = jnp.transpose(jnp.take(market_log, safe_ids, axis=0), (1, 0))]
    unnamed x10 -> x14, local copies, waits for them, and re-layouts: 4.25 us -> 4.1 us
  transfers between devices with their start and end apart: 2 -> 0, of which waited for: 2 -> 0; matrix products, arithmetic and copies ran while one was open for 5% -> 0% of each run, Pallas kernels for 0% -> 0%
where the time goes in v2:
time: 78 us; the launch traced here: 77.7 us
  Pallas kernels  70.6 us (91%)
  local copies, waits for them, and re-layouts  6.42 us (8%)
    pallas_call x1, Pallas kernels, iterate(): pl.pallas_call(functools.partial(kernel, n_mkt, n_nest, n_draw, total_dra...  70.6 us
    unnamed x14, local copies, waits for them, and re-layouts  4.1 us

profile of v2, /device:TPU:0, one launch (start us, length us, event | category | flops | bytes accessed | tf_op | source)
XLA Modules:
  0.0 77.7 jit_solution(7002722543291614821)
XLA Ops:
  0.6 0.0 copy-start
  0.7 1.2 %copy-done = bf16[32,128,128]{2,1,0:T(8,128)(2,1)S(1)} copy-done((bf16[32,128,128]{2,1,0:T(8,128)(2,1)S(1)}, bf16[32,128,128]{2,1,0:T(8,128)(2,1)}, u32[]{:S(2)}) %copy-start) | copy-done | bytes 1048600
  1.9 0.2 copy.29
  2.1 0.0 copy-start.2
  2.1 0.0 copy-start.1
  2.1 0.8 %copy-done.2 = f32[128,128]{1,0:T(8,128)S(1)} copy-done((f32[128,128]{1,0:T(8,128)S(1)}, f32[128,128]{1,0:T(8,128)}, u32[]{:S(2)}) %copy-start.2) | copy-done | bytes 65560
  2.9 0.0 copy-start.3
  2.9 0.1 copy.22
  3.0 0.6 copy-done.3
  3.6 0.1 copy.23
  3.7 0.0 copy-start.4
  3.7 0.1 reshape.28.ids_ref
  3.8 0.6 copy-done.4
  4.3 0.1 broadcast_in_dim.4.scale_ref
  4.4 0.7 copy-done.5
  5.1 0.1 copy.24.param_ref
  5.1 0.0 copy-done.1
  5.1 70.6 %iterate.1 = (f32[32,384]{1,0:T(8,128)S(1)}, f32[32,384]{1,0:T(8,128)S(1)}) custom-call(bf16[4,8,32,128]{3,2,1,0:T(8,128)(2,1)S(1)} %bitcast.15, f32[4,32,128]{2,1,0:T(8,128)S(1)} %bitcast.16, bf16[32,32,128]{2,1,0:T(8,128)(2,1)S(1)} %copy-done.1, f32[32,128]{1,0:T(8,128)S(1)} %broadcast_in_dim.4.scale_ref, s32[1,384]{1,0:T(1,128)S(1)} %reshape.28.ids_ref, ...), custom_call_target="tpu_custom_call" | custom-call | tf_op jit(solution)/shard_map/iterate/pallas_call | solution.py:289
  75.7 0.1 copy.25
  75.9 0.1 copy.26
  76.0 0.7 reshape.30
  76.7 0.1 copy.27
  76.9 0.1 copy.28
  77.0 0.7 reshape.32
  (3 shorter events, 0.0 us)
Async XLA Ops:
  0.6 1.2 %copy-start = (bf16[32,128,128]{2,1,0:T(8,128)(2,1)S(1)}, bf16[32,128,128]{2,1,0:T(8,128)(2,1)}, u32[]{:S(2)}) copy-start(bf16[32,128,128]{2,1,0:T(8,128)(2,1)} %param.6) | copy-start | bytes 3145732
  2.1 0.8 %copy-start.2 = (f32[128,128]{1,0:T(8,128)S(1)}, f32[128,128]{1,0:T(8,128)}, u32[]{:S(2)}) copy-start(f32[128,128]{1,0:T(8,128)} %param.11) | copy-start | bytes 196612
  2.1 3.1 %copy-start.1 = (bf16[32,32,128]{2,1,0:T(8,128)(2,1)S(1)}, bf16[32,32,128]{2,1,0:T(8,128)(2,1)}, u32[]{:S(2)}) copy-start(bf16[32,32,128]{2,1,0:T(8,128)(2,1)} %taste_ref.1) | copy-start | bytes 786436
  2.9 0.7 copy-start.3
  3.7 0.7 copy-start.4
  4.4 0.7 copy-start.5

commit v3 on v2

--- a/solution.py
+++ b/solution.py
@@ -11,6 +11,8 @@
 ITERS = 3
 GROUP = 8
 LANES = 128
+PACK = 4
+UNROLL = 8
 LOG2E = math.log2(math.e)
 EMPTY = -1e30
 MESH = pl.DeviceIdType.MESH
@@ -30,7 +32,7 @@
     feat_ref, log_ref, taste_ref, scale_ref, ids_ref, param_ref,
     value_ref, share_ref,
     x_ref, logm_ref, onehot_ref, s_ref, target_ref, live_col_ref,
-    mu_ref, u_ref, inner_ref, incl_ref, hi_ref, lo_ref, spread_ref, pick_ref, vcat_ref,
+    mu_ref, u_ref, inner_ref, incl_ref, taste_ref2, shift_ref, sums_ref,
     tot_send, tot_recv, part_send, part_recv,
     own_sem, z_ssem, z_rsem, log_ssem, log_rsem, x_ssem, x_rsem, c_ssem, c_rsem,
     tot_ssem, tot_rsem, part_ssem, part_rsem,
@@ -116,13 +118,7 @@
             send_sem=part_ssem.at[it, ch, k], recv_sem=part_rsem.at[it, ch, k],
             device_id={"draw": draw_peers[k]}, device_id_type=MESH)
 
-    row = lax.broadcasted_iota(jnp.int32, (LANES, draws), 0)
-    lane = lax.broadcasted_iota(jnp.int32, (draws, LANES), 1)
-    for i in range(GROUP):
-        mine = (row == i) | (row == GROUP + i) | (row == 2 * GROUP + i)
-        spread_ref[i] = jnp.where(mine, 1.0, 0.0).astype(BF16)
-        pick_ref[i * draws:(i + 1) * draws, :] = jnp.where(lane == i, 1.0, 0.0).astype(BF16)
-
+    lane = lax.broadcasted_iota(jnp.int32, (nests, LANES), 1)
     ids = ids_ref[...]
     live_row = jnp.where(ids >= 0, 1.0, 0.0)
     live_col_ref[...] = jnp.broadcast_to(live_row, (draws, cols)).T
@@ -158,16 +154,26 @@
             else:
                 s_ref[w] += piece
 
-    def mu_step(m, _):
-        rows = pl.ds(m, depth, stride=markets)
-        sx = jnp.concatenate([s_ref.at[w][rows, :] for w in range(cols // LANES)], axis=1).astype(BF16)
-        taste = (scale_ref[...] * taste_ref[m].astype(F32)).astype(BF16)
-        mu = lax.dot_general(sx, taste, (((0,), (0,)), ((), ())), preferred_element_type=F32)
-        mu = (mu.reshape(slots, nests, draws) * scale_col[None]).reshape(cols, draws)
-        mu_ref[m] = jnp.where(live_col_ref[...] > 0.0, mu, EMPTY)
+    taste_ref2[...] = jnp.zeros_like(taste_ref2)
+
+    def mu_step(step, _):
+        first = step * PACK
+        rows = [pl.ds(first + j, depth, stride=markets) for j in range(PACK)]
+        sx = jnp.concatenate(
+            [jnp.concatenate([s_ref.at[w][at, :] for at in rows], axis=0).T
+             for w in range(cols // LANES)], axis=0).astype(BF16)
+        for j in range(PACK):
+            taste = (scale_ref[...] * taste_ref[first + j].astype(F32)).astype(BF16)
+            taste_ref2[j * depth:(j + 1) * depth, j * draws:(j + 1) * draws] = taste
+        mu = jnp.dot(sx, taste_ref2[...], preferred_element_type=F32)
+        live = live_col_ref[...] > 0.0
+        for j in range(PACK):
+            part = mu[:, j * draws:(j + 1) * draws]
+            part = (part.reshape(slots, nests, draws) * scale_col[None]).reshape(cols, draws)
+            mu_ref[first + j] = jnp.where(live, part, EMPTY)
         return 0
 
-    lax.fori_loop(0, markets, mu_step, 0)
+    lax.fori_loop(0, markets // PACK, mu_step, 0)
 
     own_log.wait()
     for d in range(1, n_mkt):
@@ -183,48 +189,55 @@
     value_ref[...] = jnp.where(live_row > 0.0, target - jnp.log(1.0 - inside), 0.0)
 
     def utilities(it, ch, value):
-        parts = split3(value * scale_row)
-        stacked = jnp.concatenate(
-            list(parts) + [jnp.zeros((LANES - 3 * GROUP, cols), F32)], axis=0)
-        vcat_ref[...] = stacked.T.astype(BF16)
-
-        def body(i, _):
-            m = ch * GROUP + i
-            shift = jnp.dot(vcat_ref[...], spread_ref[i], preferred_element_type=F32)
-            u = jnp.exp2(mu_ref[m] + shift)
-            u_ref[m] = u
-            inner = jnp.sum(u.reshape(slots, nests, draws), axis=0)
-            incl = jnp.exp(rate_col * jnp.log(inner))
-            inner_ref[m] = inner
-            incl_ref[m] = incl
-            tot_send[it, ch, pl.ds(i, 1), :] = jnp.sum(incl, axis=0, keepdims=True)
+        pad = jnp.zeros((LANES - GROUP, cols), F32)
+        shift_ref[...] = jnp.concatenate([value * scale_row, pad], axis=0).T
+
+        def body(step, inner):
+            inner = list(inner)
+            for j in range(UNROLL):
+                rows = pl.ds(pl.multiple_of((step * UNROLL + j) * nests, nests), nests)
+                shift = shift_ref[rows, :]
+                for i in range(GROUP):
+                    m = ch * GROUP + i
+                    u = jnp.exp2(mu_ref[m, rows, :] + shift[:, i:i + 1])
+                    u_ref[m, rows, :] = u
+                    inner[i] = inner[i] + u
+            return tuple(inner)
+
+        zero = jnp.zeros((nests, draws), F32)
+        inner = lax.fori_loop(0, slots // UNROLL, body, (zero,) * GROUP)
+        totals = []
+        for i in range(GROUP):
+            incl = jnp.exp(rate_col * jnp.log(inner[i]))
+            inner_ref[ch * GROUP + i] = inner[i]
+            incl_ref[ch * GROUP + i] = incl
+            totals.append(jnp.sum(incl, axis=0, keepdims=True))
+        tot_send[it, ch] = jnp.concatenate(totals, axis=0)
+        for k in range(n_nest - 1):
+            tot_copy(it, ch, k).start()
+
+    def shares(it, ch):
+        for k in range(n_nest - 1):
+            tot_copy(it, ch, k).wait_recv()
+
+        total = 1.0 + tot_send[it, ch]
+        for k in range(n_nest - 1):
+            total = total + tot_recv[it, ch, k]
+        ratio = [incl_ref[ch * GROUP + i] / (inner_ref[ch * GROUP + i] * total[i:i + 1])
+                 for i in range(GROUP)]
+
+        def body(step, _):
+            for j in range(UNROLL):
+                rows = pl.ds(pl.multiple_of((step * UNROLL + j) * nests, nests), nests)
+                sums = jnp.zeros((nests, LANES), F32)
+                for i in range(GROUP):
+                    p = u_ref[ch * GROUP + i, rows, :] * ratio[i]
+                    sums = jnp.where(lane == i, jnp.sum(p, axis=1, keepdims=True), sums)
+                sums_ref[rows, :] = sums
             return 0
 
-        lax.fori_loop(0, GROUP, body, 0)
-        for k in range(n_nest - 1):
-            tot_copy(it, ch, k).start()
-
-    def shares(it, ch):
-        for k in range(n_nest - 1):
-            tot_copy(it, ch, k).wait_recv()
-
-        def body(i, _):
-            m = ch * GROUP + i
-            total = 1.0 + tot_send[it, ch, pl.ds(i, 1), :]
-            for k in range(n_nest - 1):
-                total = total + tot_recv[it, ch, k, pl.ds(i, 1), :]
-            ratio = incl_ref[m] / (inner_ref[m] * total)
-            p = (u_ref[m].reshape(slots, nests, draws) * ratio[None]).reshape(cols, draws)
-            hi = p.astype(BF16)
-            at = pl.ds(pl.multiple_of(i * draws, draws), draws)
-            hi_ref[:, at] = hi
-            lo_ref[:, at] = (p - hi.astype(F32)).astype(BF16)
-            return 0
-
-        lax.fori_loop(0, GROUP, body, 0)
-        out = jnp.dot(hi_ref[...], pick_ref[...], preferred_element_type=F32)
-        out = out + jnp.dot(lo_ref[...], pick_ref[...], preferred_element_type=F32)
-        part_send[it, ch] = out.T[:GROUP]
+        lax.fori_loop(0, slots // UNROLL, body, 0)
+        part_send[it, ch] = sums_ref[...].T[:GROUP]
         for k in range(n_draw - 1):
             part_copy(it, ch, k).start()
 
@@ -302,11 +315,9 @@
             pltpu.VMEM((markets, cols, draws), F32),
             pltpu.VMEM((markets, nests, draws), F32),
             pltpu.VMEM((markets, nests, draws), F32),
-            pltpu.VMEM((cols, GROUP * draws), BF16),
-            pltpu.VMEM((cols, GROUP * draws), BF16),
-            pltpu.VMEM((GROUP, LANES, draws), BF16),
-            pltpu.VMEM((GROUP * draws, LANES), BF16),
-            pltpu.VMEM((cols, LANES), BF16),
+            pltpu.VMEM((PACK * depth, PACK * draws), BF16),
+            pltpu.VMEM((cols, LANES), F32),
+            pltpu.VMEM((cols, LANES), F32),
             pltpu.VMEM((ITERS, chunks, GROUP, draws), F32),
             pltpu.VMEM((ITERS, chunks, n_nest - 1, GROUP, draws), F32),
             pltpu.VMEM((ITERS, chunks, GROUP, cols), F32),

time: 78 us -> 63.3 us (0.81)
  Pallas kernels: 70.6 us -> 55.9 us
    pallas_call x1, Pallas kernels: 70.6 us -> 55.9 us  [iterate(): pl.pallas_call(functools.partial(kernel, n_mkt, n_nest, n_draw, total_dra...]
where the time goes in v3:
time: 63.3 us; the launch traced here: 63.1 us
  Pallas kernels  55.9 us (88%)
  local copies, waits for them, and re-layouts  6.42 us (10%)
  between operations  0.74 us (1%)
    pallas_call x1, Pallas kernels, iterate(): pl.pallas_call(functools.partial(kernel, n_mkt, n_nest, n_draw, total_dra...  55.9 us
    unnamed x14, local copies, waits for them, and re-layouts  4.1 us
    reshape x2, local copies, waits for them, and re-layouts, order(): x.reshape(markets, slots, nests).transpose(0, 2, 1)  1.44 us

profile of v3, /device:TPU:0, one launch (start us, length us, event | category | flops | bytes accessed | tf_op | source)
XLA Modules:
  0.0 63.1 jit_solution(2526039549681940045)
XLA Ops:
  0.6 0.0 copy-start
  0.7 1.2 %copy-done = bf16[32,128,128]{2,1,0:T(8,128)(2,1)S(1)} copy-done((bf16[32,128,128]{2,1,0:T(8,128)(2,1)S(1)}, bf16[32,128,128]{2,1,0:T(8,128)(2,1)}, u32[]{:S(2)}) %copy-start) | copy-done | bytes 1048600
  1.9 0.2 copy.29
  2.1 0.0 copy-start.2
  2.1 0.0 copy-start.1
  2.1 0.8 %copy-done.2 = f32[128,128]{1,0:T(8,128)S(1)} copy-done((f32[128,128]{1,0:T(8,128)S(1)}, f32[128,128]{1,0:T(8,128)}, u32[]{:S(2)}) %copy-start.2) | copy-done | bytes 65560
  2.9 0.0 copy-start.3
  2.9 0.1 copy.22
  3.0 0.6 copy-done.3
  3.6 0.1 copy.23
  3.7 0.0 copy-start.4
  3.7 0.1 reshape.28.ids_ref
  3.8 0.6 copy-done.4
  4.3 0.1 broadcast_in_dim.4.scale_ref
  4.4 0.7 %copy-done.5 = f32[8]{0:T(128)S(1)} copy-done((f32[8]{0:T(128)S(1)}, f32[8]{0:T(128)}, u32[]{:S(2)}) %copy-start.5) | copy-done | bytes 56
  5.1 0.1 copy.24.param_ref
  5.1 0.0 copy-done.1
  5.1 55.9 %iterate.1 = (f32[32,384]{1,0:T(8,128)S(1)}, f32[32,384]{1,0:T(8,128)S(1)}) custom-call(bf16[4,8,32,128]{3,2,1,0:T(8,128)(2,1)S(1)} %bitcast.15, f32[4,32,128]{2,1,0:T(8,128)S(1)} %bitcast.16, bf16[32,32,128]{2,1,0:T(8,128)(2,1)S(1)} %copy-done.1, f32[32,128]{1,0:T(8,128)S(1)} %broadcast_in_dim.4.scale_ref, s32[1,384]{1,0:T(1,128)S(1)} %reshape.28.ids_ref, ...), custom_call_target="tpu_custom_call" | custom-call | tf_op jit(solution)/shard_map/iterate/pallas_call | solution.py:302
  61.1 0.1 copy.25
  61.2 0.1 copy.26
  61.3 0.7 %reshape.30 = f32[32,384]{1,0:T(8,128)} reshape(f32[32,8,48]{2,1,0:T(8,128)S(1)} %copy.26) | data formatting | bytes 98304 | tf_op jit(solution)/shard_map/reshape | solution.py:356
  62.1 0.1 copy.27
  62.2 0.1 copy.28
  62.3 0.7 %reshape.32 = f32[32,384]{1,0:T(8,128)} reshape(f32[32,8,48]{2,1,0:T(8,128)S(1)} %copy.28) | data formatting | bytes 98304 | tf_op jit(solution)/shard_map/reshape | solution.py:356
  (3 shorter events, 0.0 us)
Async XLA Ops:
  0.6 1.2 %copy-start = (bf16[32,128,128]{2,1,0:T(8,128)(2,1)S(1)}, bf16[32,128,128]{2,1,0:T(8,128)(2,1)}, u32[]{:S(2)}) copy-start(bf16[32,128,128]{2,1,0:T(8,128)(2,1)} %param.6) | copy-start | bytes 3145732
  2.1 0.8 %copy-start.2 = (f32[128,128]{1,0:T(8,128)S(1)}, f32[128,128]{1,0:T(8,128)}, u32[]{:S(2)}) copy-start(f32[128,128]{1,0:T(8,128)} %param.11) | copy-start | bytes 196612
  2.1 3.1 %copy-start.1 = (bf16[32,32,128]{2,1,0:T(8,128)(2,1)S(1)}, bf16[32,32,128]{2,1,0:T(8,128)(2,1)}, u32[]{:S(2)}) copy-start(bf16[32,32,128]{2,1,0:T(8,128)(2,1)} %taste_ref.1) | copy-start | bytes 786436
  2.9 0.7 %copy-start.3 = (s32[8,48]{1,0:T(8,128)S(1)}, s32[8,48]{1,0:T(8,128)}, u32[]{:S(2)}) copy-start(s32[8,48]{1,0:T(8,128)} %param.10) | copy-start | bytes 4612
  3.7 0.7 %copy-start.4 = (f32[32]{0:T(128)S(1)}, f32[32]{0:T(128)}, u32[]{:S(2)}) copy-start(f32[32]{0:T(128)} %param.8) | copy-start | bytes 388
  4.4 0.7 %copy-start.5 = (f32[8]{0:T(128)S(1)}, f32[8]{0:T(128)}, u32[]{:S(2)}) copy-start(f32[8]{0:T(128)} %param.9) | copy-start | bytes 100

commit v4 on v3

--- a/solution.py
+++ b/solution.py
@@ -12,7 +12,6 @@
 GROUP = 8
 LANES = 128
 PACK = 4
-UNROLL = 8
 LOG2E = math.log2(math.e)
 EMPTY = -1e30
 MESH = pl.DeviceIdType.MESH
@@ -194,18 +193,19 @@
 
         def body(step, inner):
             inner = list(inner)
-            for j in range(UNROLL):
-                rows = pl.ds(pl.multiple_of((step * UNROLL + j) * nests, nests), nests)
-                shift = shift_ref[rows, :]
-                for i in range(GROUP):
-                    m = ch * GROUP + i
-                    u = jnp.exp2(mu_ref[m, rows, :] + shift[:, i:i + 1])
-                    u_ref[m, rows, :] = u
+            rows = [pl.ds(pl.multiple_of((step * slots + j) * nests, nests), nests)
+                    for j in range(slots)]
+            shifts = [shift_ref[at, :] for at in rows]
+            for i in range(GROUP):
+                m = ch * GROUP + i
+                for at, shift in zip(rows, shifts):
+                    u = jnp.exp2(mu_ref[m, at, :] + shift[:, i:i + 1])
+                    u_ref[m, at, :] = u
                     inner[i] = inner[i] + u
             return tuple(inner)
 
         zero = jnp.zeros((nests, draws), F32)
-        inner = lax.fori_loop(0, slots // UNROLL, body, (zero,) * GROUP)
+        inner = lax.fori_loop(0, slots // slots, body, (zero,) * GROUP)
         totals = []
         for i in range(GROUP):
             incl = jnp.exp(rate_col * jnp.log(inner[i]))
@@ -227,8 +227,8 @@
                  for i in range(GROUP)]
 
         def body(step, _):
-            for j in range(UNROLL):
-                rows = pl.ds(pl.multiple_of((step * UNROLL + j) * nests, nests), nests)
+            for j in range(slots):
+                rows = pl.ds(pl.multiple_of((step * slots + j) * nests, nests), nests)
                 sums = jnp.zeros((nests, LANES), F32)
                 for i in range(GROUP):
                     p = u_ref[ch * GROUP + i, rows, :] * ratio[i]
@@ -236,7 +236,7 @@
                 sums_ref[rows, :] = sums
             return 0
 
-        lax.fori_loop(0, slots // UNROLL, body, 0)
+        lax.fori_loop(0, slots // slots, body, 0)
         part_send[it, ch] = sums_ref[...].T[:GROUP]
         for k in range(n_draw - 1):
             part_copy(it, ch, k).start()

time: 63.3 us -> 55.3 us (0.87)
  Pallas kernels: 55.9 us -> 47.9 us
    pallas_call x1, Pallas kernels: 55.9 us -> 47.9 us  [iterate(): pl.pallas_call(functools.partial(kernel, n_mkt, n_nest, n_draw, total_dra...]
where the time goes in v4:
time: 55.3 us; the launch traced here: 55.1 us
  Pallas kernels  47.9 us (87%)
  local copies, waits for them, and re-layouts  6.42 us (12%)
  between operations  0.74 us (1%)
    pallas_call x1, Pallas kernels, iterate(): pl.pallas_call(functools.partial(kernel, n_mkt, n_nest, n_draw, total_dra...  47.9 us
    unnamed x14, local copies, waits for them, and re-layouts  4.1 us
    reshape x2, local copies, waits for them, and re-layouts, order(): x.reshape(markets, slots, nests).transpose(0, 2, 1)  1.44 us

profile of v4, /device:TPU:0, one launch (start us, length us, event | category | flops | bytes accessed | tf_op | source)
XLA Modules:
  0.0 55.1 jit_solution(1476140533553697706)
XLA Ops:
  0.6 0.0 copy-start
  0.7 1.2 %copy-done = bf16[32,128,128]{2,1,0:T(8,128)(2,1)S(1)} copy-done((bf16[32,128,128]{2,1,0:T(8,128)(2,1)S(1)}, bf16[32,128,128]{2,1,0:T(8,128)(2,1)}, u32[]{:S(2)}) %copy-start) | copy-done | bytes 1048600
  1.9 0.2 copy.29
  2.1 0.0 copy-start.2
  2.1 0.0 copy-start.1
  2.1 0.8 %copy-done.2 = f32[128,128]{1,0:T(8,128)S(1)} copy-done((f32[128,128]{1,0:T(8,128)S(1)}, f32[128,128]{1,0:T(8,128)}, u32[]{:S(2)}) %copy-start.2) | copy-done | bytes 65560
  2.9 0.0 copy-start.3
  2.9 0.1 copy.22
  3.0 0.6 %copy-done.3 = s32[8,48]{1,0:T(8,128)S(1)} copy-done((s32[8,48]{1,0:T(8,128)S(1)}, s32[8,48]{1,0:T(8,128)}, u32[]{:S(2)}) %copy-start.3) | copy-done | bytes 1560
  3.6 0.1 copy.23
  3.7 0.0 copy-start.4
  3.7 0.1 reshape.28.ids_ref
  3.8 0.6 %copy-done.4 = f32[32]{0:T(128)S(1)} copy-done((f32[32]{0:T(128)S(1)}, f32[32]{0:T(128)}, u32[]{:S(2)}) %copy-start.4) | copy-done | bytes 152
  4.3 0.1 broadcast_in_dim.4.scale_ref
  4.4 0.7 %copy-done.5 = f32[8]{0:T(128)S(1)} copy-done((f32[8]{0:T(128)S(1)}, f32[8]{0:T(128)}, u32[]{:S(2)}) %copy-start.5) | copy-done | bytes 56
  5.1 0.1 copy.24.param_ref
  5.1 0.0 copy-done.1
  5.1 47.9 %iterate.1 = (f32[32,384]{1,0:T(8,128)S(1)}, f32[32,384]{1,0:T(8,128)S(1)}) custom-call(bf16[4,8,32,128]{3,2,1,0:T(8,128)(2,1)S(1)} %bitcast.15, f32[4,32,128]{2,1,0:T(8,128)S(1)} %bitcast.16, bf16[32,32,128]{2,1,0:T(8,128)(2,1)S(1)} %copy-done.1, f32[32,128]{1,0:T(8,128)S(1)} %broadcast_in_dim.4.scale_ref, s32[1,384]{1,0:T(1,128)S(1)} %reshape.28.ids_ref, ...), custom_call_target="tpu_custom_call" | custom-call | tf_op jit(solution)/shard_map/iterate/pallas_call | solution.py:302
  53.1 0.1 copy.25
  53.2 0.1 copy.26
  53.4 0.7 %reshape.30 = f32[32,384]{1,0:T(8,128)} reshape(f32[32,8,48]{2,1,0:T(8,128)S(1)} %copy.26) | data formatting | bytes 98304 | tf_op jit(solution)/shard_map/reshape | solution.py:356
  54.1 0.1 copy.27
  54.2 0.1 copy.28
  54.4 0.7 %reshape.32 = f32[32,384]{1,0:T(8,128)} reshape(f32[32,8,48]{2,1,0:T(8,128)S(1)} %copy.28) | data formatting | bytes 98304 | tf_op jit(solution)/shard_map/reshape | solution.py:356
  (3 shorter events, 0.0 us)
Async XLA Ops:
  0.6 1.2 %copy-start = (bf16[32,128,128]{2,1,0:T(8,128)(2,1)S(1)}, bf16[32,128,128]{2,1,0:T(8,128)(2,1)}, u32[]{:S(2)}) copy-start(bf16[32,128,128]{2,1,0:T(8,128)(2,1)} %param.6) | copy-start | bytes 3145732
  2.1 0.8 %copy-start.2 = (f32[128,128]{1,0:T(8,128)S(1)}, f32[128,128]{1,0:T(8,128)}, u32[]{:S(2)}) copy-start(f32[128,128]{1,0:T(8,128)} %param.11) | copy-start | bytes 196612
  2.1 3.1 %copy-start.1 = (bf16[32,32,128]{2,1,0:T(8,128)(2,1)S(1)}, bf16[32,32,128]{2,1,0:T(8,128)(2,1)}, u32[]{:S(2)}) copy-start(bf16[32,32,128]{2,1,0:T(8,128)(2,1)} %taste_ref.1) | copy-start | bytes 786436
  2.9 0.7 %copy-start.3 = (s32[8,48]{1,0:T(8,128)S(1)}, s32[8,48]{1,0:T(8,128)}, u32[]{:S(2)}) copy-start(s32[8,48]{1,0:T(8,128)} %param.10) | copy-start | bytes 4612
  3.7 0.7 %copy-start.4 = (f32[32]{0:T(128)S(1)}, f32[32]{0:T(128)}, u32[]{:S(2)}) copy-start(f32[32]{0:T(128)} %param.8) | copy-start | bytes 388
  4.4 0.7 %copy-start.5 = (f32[8]{0:T(128)S(1)}, f32[8]{0:T(128)}, u32[]{:S(2)}) copy-start(f32[8]{0:T(128)} %param.9) | copy-start | bytes 100
